TPU v7x, 32 devices: a whole 2x2x4 slice. The times are simulated.
32 devices in a mesh: tensor: 2 (over x), batch: 4 (over y, core), context: 4 (over z).
Axes of the slice: x: 2, y: 2, z: 4, core: 2. Of those that a mesh axis runs over, the one named last changes fastest.
Arguments:
- block_input: bfloat16 [4, 1024, 2048], P('batch', 'context'), may hold values from -6 to 6
- gain_first: float32 [2048], replicated, may hold values from 0.1 to 1.9
- shift_first: float32 [2048], replicated, may hold values from -3 to 3
- attend_weight: bfloat16 [2048, 3, 2048], P(None, None, 'tensor'), may hold values from -0.125 to 0.125
- attend_offset: float32 [2, 2048], P(None, 'tensor'), may hold values from -1 to 1
- merge_weight: bfloat16 [2048, 2048], P('tensor'), may hold values from -1.5 to 1.5
- merge_offset: float32 [2048], replicated, may hold values from -3 to 3
- gain_second: float32 [2048], replicated, may hold values from 0.1 to 1.9
- shift_second: float32 [2048], replicated, may hold values from -3 to 3
- expand_weight: bfloat16 [2048, 8192], P(None, 'tensor'), may hold values from -0.125 to 0.125
- expand_offset: float32 [8192], P('tensor'), may hold values from -3 to 3
- reduce_weight: bfloat16 [8192, 2048], P('tensor'), may hold values from -0.0625 to 0.0625
- reduce_offset: float32 [2048], replicated, may hold values from -3 to 3
- key_mask: int32 [4, 1024], P('batch', 'context'), may hold values 0 or 1
- true_lengths: int32 [4], P('batch'), may hold values from 512 to 1024, as said below
- output_cotangent: bfloat16 [4, 1024, 2048], P('batch', 'context'), may hold values from -6 to 6
Outputs:
- block_output: bfloat16 [4, 1024, 2048], P('batch', 'context')
- input_gradient: bfloat16 [4, 1024, 2048], P('batch', 'context')
- gain_first_gradient: float32 [2048], replicated
- shift_first_gradient: float32 [2048], replicated
- attend_weight_gradient: float32 [2048, 3, 2048], P(('batch', 'context'), None, 'tensor')
- attend_offset_gradient: float32 [2, 2048], P(None, 'tensor')
- merge_weight_gradient: float32 [2048, 2048], P('tensor', ('batch', 'context'))
- merge_offset_gradient: float32 [2048], replicated
- gain_second_gradient: float32 [2048], replicated
- shift_second_gradient: float32 [2048], replicated
- expand_weight_gradient: float32 [2048, 8192], P(('batch', 'context'), 'tensor')
- expand_offset_gradient: float32 [8192], P('tensor')
- reduce_weight_gradient: float32 [8192, 2048], P('tensor', ('batch', 'context'))
- reduce_offset_gradient: float32 [2048], replicated
Inputs may be any that keep to these rules, and one draw needn't show every extreme that they name: `true_lengths`: rows at or past a sequence's true length are padding; some sequence fills all 1024 slots in every draw.
All inputs are finite; a program needn't handle non-finite values. No bound on the sum of `key_mask` on one device may be relied on, other than what follows from the above.
Results may differ from a plain program's by a relative error of at most 0.02.
Values may be sent and summed in bfloat16 or wider, within the bound.
A program may use at most 256 MiB of HBM per device.

v0:
```python
import jax
import jax.numpy as jnp
from jax import lax
from jax.sharding import PartitionSpec as P

HEAD_DIM = 128


EPS = 1e-05
NEGATIVE = -1e30


def norm_parts(values, gain, shift):
    average = jnp.mean(values, -1, keepdims=True)
    center = values - average
    inverse = lax.rsqrt(jnp.mean(center * center, -1, keepdims=True) + EPS)
    normal = center * inverse
    return (normal * gain + shift, normal, inverse)


def norm_back(upstream, normal, inverse, gain):
    gain_part = jnp.sum(upstream * normal, (0, 1))
    shift_part = jnp.sum(upstream, (0, 1))
    scaled = upstream * gain
    inner = (
        scaled
        - jnp.mean(scaled, -1, keepdims=True)
        - normal * jnp.mean(scaled * normal, -1, keepdims=True)
    )
    return (inverse * inner, gain_part, shift_part)


def allowed_mask(query_pos, key_pos, key_flags):
    causal = key_pos[None, :] <= query_pos[:, None]
    itself = key_pos[None, :] == query_pos[:, None]
    return causal[None, None] & ((key_flags[:, None, None, :] > 0.5) | itself[None, None])


def masked_scores(query_heads, key_heads, allowed, scale):
    raw = (
        jnp.einsum("sqhe,skhe->shqk", query_heads, key_heads, preferred_element_type=jnp.float32)
        * scale
    )
    return jnp.where(allowed, raw, NEGATIVE)


def gelu_tanh(values):
    return jax.nn.gelu(values, approximate=True)


def tensor_total(values):
    return lax.psum(values.astype(jnp.bfloat16), "tensor").astype(jnp.float32)


def local(
    block_input,
    gain_first,
    shift_first,
    attend_weight,
    attend_offset,
    merge_weight,
    merge_offset,
    gain_second,
    shift_second,
    expand_weight,
    expand_offset,
    reduce_weight,
    reduce_offset,
    key_mask,
    true_lengths,
    output_cotangent,
):
    seq_count, block_len, width = block_input.shape
    local_width = attend_weight.shape[2]
    head_size = HEAD_DIM
    local_heads = local_width // head_size
    scale = head_size ** (-0.5)
    full_len = block_len * lax.axis_size("context")
    query_pos = lax.axis_index("context") * block_len + jnp.arange(block_len, dtype=jnp.int32)
    key_pos = jnp.arange(full_len, dtype=jnp.int32)

    def heads_of(values):
        return values.reshape(values.shape[0], values.shape[1], local_heads, head_size)

    inputs = block_input.astype(jnp.float32)
    normed, normal_one, inverse_one = norm_parts(inputs, gain_first, shift_first)
    normed = normed.astype(jnp.bfloat16)
    triple = jnp.einsum("std,dch->csth", normed, attend_weight, preferred_element_type=jnp.float32)
    queries = (triple[0] + attend_offset[0]).astype(jnp.bfloat16)
    keys_own = triple[1].astype(jnp.bfloat16)
    values_own = (triple[2] + attend_offset[1]).astype(jnp.bfloat16)
    row_live = query_pos[None, :] < true_lengths[:, None]
    key_flags = ((key_mask == 1) & row_live).astype(jnp.bfloat16)
    keys_all, values_all, flags_all = (
        lax.all_gather(keys_own, "context", axis=1, tiled=True),
        lax.all_gather(values_own, "context", axis=1, tiled=True),
        lax.all_gather(key_flags, "context", axis=1, tiled=True),
    )
    query_heads = heads_of(queries)
    key_heads = heads_of(keys_all)
    value_heads = heads_of(values_all)
    allowed = allowed_mask(query_pos, key_pos, flags_all)
    scores = masked_scores(query_heads, key_heads, allowed, scale)
    top_score = jnp.max(scores, -1, keepdims=True)
    log_total = top_score + jnp.log(jnp.sum(jnp.exp(scores - top_score), -1, keepdims=True))
    weights = jnp.exp(scores - log_total)
    weights_low = weights.astype(jnp.bfloat16)
    mixed = jnp.einsum(
        "shqk,skhe->sqhe", weights_low, value_heads, preferred_element_type=jnp.float32
    )
    mixed = mixed.reshape(seq_count, block_len, local_width).astype(jnp.bfloat16)
    attended_part = jnp.einsum(
        "sth,hd->std", mixed, merge_weight, preferred_element_type=jnp.float32
    )
    middle = inputs + tensor_total(attended_part) + merge_offset
    normed_two, normal_two, inverse_two = norm_parts(middle, gain_second, shift_second)
    normed_two = normed_two.astype(jnp.bfloat16)
    hidden = (
        jnp.einsum("std,df->stf", normed_two, expand_weight, preferred_element_type=jnp.float32)
        + expand_offset
    )
    active, gelu_back = jax.vjp(gelu_tanh, hidden)
    active_low = active.astype(jnp.bfloat16)
    reduced_part = jnp.einsum(
        "stf,fd->std", active_low, reduce_weight, preferred_element_type=jnp.float32
    )
    block_output = (middle + tensor_total(reduced_part) + reduce_offset).astype(jnp.bfloat16)
    upstream = output_cotangent.astype(jnp.float32) * row_live.astype(jnp.float32)[:, :, None]
    upstream_low = upstream.astype(jnp.bfloat16)
    reduce_grad = jnp.einsum(
        "stf,std->fd", active_low, upstream_low, preferred_element_type=jnp.float32
    )
    reduce_off_grad = jnp.sum(upstream, (0, 1))
    active_grad = jnp.einsum(
        "std,fd->stf", upstream_low, reduce_weight, preferred_element_type=jnp.float32
    )
    hidden_grad = gelu_back(active_grad)[0].astype(jnp.bfloat16)
    expand_off_grad = jnp.sum(hidden_grad.astype(jnp.float32), (0, 1))
    expand_grad = jnp.einsum(
        "std,stf->df", normed_two, hidden_grad, preferred_element_type=jnp.float32
    )
    second_part = jnp.einsum(
        "stf,df->std", hidden_grad, expand_weight, preferred_element_type=jnp.float32
    )
    middle_part, gain_two_grad, shift_two_grad = norm_back(
        tensor_total(second_part), normal_two, inverse_two, gain_second
    )
    middle_grad = upstream + middle_part
    middle_low = middle_grad.astype(jnp.bfloat16)
    merge_off_grad = jnp.sum(middle_grad, (0, 1))
    merge_grad = jnp.einsum("sth,std->hd", mixed, middle_low, preferred_element_type=jnp.float32)
    mixed_grad = jnp.einsum(
        "std,hd->sth", middle_low, merge_weight, preferred_element_type=jnp.float32
    ).astype(jnp.bfloat16)
    mixed_heads = heads_of(mixed_grad)
    scores = masked_scores(query_heads, key_heads, allowed, scale)
    weights = jnp.exp(scores - log_total)
    weights_grad = jnp.einsum(
        "sqhe,skhe->shqk", mixed_heads, value_heads, preferred_element_type=jnp.float32
    )
    row_dot = jnp.sum(weights * weights_grad, -1, keepdims=True)
    score_grad = (weights * (weights_grad - row_dot)).astype(jnp.bfloat16)
    query_grad = (
        jnp.einsum("shqk,skhe->sqhe", score_grad, key_heads, preferred_element_type=jnp.float32)
        * scale
    )
    query_grad = query_grad.reshape(seq_count, block_len, local_width).astype(jnp.bfloat16)
    key_part = (
        jnp.einsum("shqk,sqhe->skhe", score_grad, query_heads, preferred_element_type=jnp.float32)
        * scale
    )
    value_part = jnp.einsum(
        "shqk,sqhe->skhe",
        weights.astype(jnp.bfloat16),
        mixed_heads,
        preferred_element_type=jnp.float32,
    )
    key_sum, value_sum = (
        lax.psum_scatter(
            key_part.reshape(seq_count, full_len, local_width).astype(jnp.bfloat16),
            "context",
            scatter_dimension=1,
            tiled=True,
        ).astype(jnp.float32),
        lax.psum_scatter(
            value_part.reshape(seq_count, full_len, local_width).astype(jnp.bfloat16),
            "context",
            scatter_dimension=1,
            tiled=True,
        ).astype(jnp.float32),
    )
    key_low = key_sum.astype(jnp.bfloat16)
    value_low = value_sum.astype(jnp.bfloat16)
    offset_grad = jnp.stack(
        [
            jnp.sum(query_grad.astype(jnp.float32), (0, 1)),
            jnp.sum(value_low.astype(jnp.float32), (0, 1)),
        ]
    )
    triple_grad = jnp.stack([query_grad, key_low, value_low])
    attend_grad = jnp.einsum(
        "std,csth->dch", normed, triple_grad, preferred_element_type=jnp.float32
    )
    first_part = jnp.einsum(
        "csth,dch->std", triple_grad, attend_weight, preferred_element_type=jnp.float32
    )
    input_part, gain_one_grad, shift_one_grad = norm_back(
        tensor_total(first_part), normal_one, inverse_one, gain_first
    )
    input_gradient = (middle_grad + input_part).astype(jnp.bfloat16)
    attend_total, expand_total = (
        lax.psum_scatter(
            attend_grad.astype(jnp.bfloat16), ("batch", "context"), scatter_dimension=0, tiled=True
        ).astype(jnp.float32),
        lax.psum_scatter(
            expand_grad.astype(jnp.bfloat16), ("batch", "context"), scatter_dimension=0, tiled=True
        ).astype(jnp.float32),
    )
    merge_total, reduce_total = (
        lax.psum_scatter(
            merge_grad.astype(jnp.bfloat16), ("batch", "context"), scatter_dimension=1, tiled=True
        ).astype(jnp.float32),
        lax.psum_scatter(
            reduce_grad.astype(jnp.bfloat16), ("batch", "context"), scatter_dimension=1, tiled=True
        ).astype(jnp.float32),
    )
    smalls = (
        lax.psum(gain_one_grad.astype(jnp.bfloat16), ("batch", "context")).astype(jnp.float32),
        lax.psum(shift_one_grad.astype(jnp.bfloat16), ("batch", "context")).astype(jnp.float32),
        lax.psum(offset_grad.astype(jnp.bfloat16), ("batch", "context")).astype(jnp.float32),
        lax.psum(merge_off_grad.astype(jnp.bfloat16), ("batch", "context")).astype(jnp.float32),
        lax.psum(gain_two_grad.astype(jnp.bfloat16), ("batch", "context")).astype(jnp.float32),
        lax.psum(shift_two_grad.astype(jnp.bfloat16), ("batch", "context")).astype(jnp.float32),
        lax.psum(expand_off_grad.astype(jnp.bfloat16), ("batch", "context")).astype(jnp.float32),
        lax.psum(reduce_off_grad.astype(jnp.bfloat16), ("batch", "context")).astype(jnp.float32),
    )
    return (
        block_output,
        input_gradient,
        smalls[0],
        smalls[1],
        attend_total,
        smalls[2],
        merge_total,
        smalls[3],
        smalls[4],
        smalls[5],
        expand_total,
        smalls[6],
        reduce_total,
        smalls[7],
    )


def solution(mesh):
    return jax.shard_map(
        local,
        mesh=mesh,
        in_specs=(
            P("batch", "context", None),
            P(),
            P(),
            P(None, None, "tensor"),
            P(None, "tensor"),
            P("tensor", None),
            P(),
            P(),
            P(),
            P(None, "tensor"),
            P("tensor"),
            P("tensor", None),
            P(),
            P("batch", "context"),
            P("batch"),
            P("batch", "context", None),
        ),
        out_specs=(
            P("batch", "context", None),
            P("batch", "context", None),
            P(),
            P(),
            P(("batch", "context"), None, "tensor"),
            P(None, "tensor"),
            P("tensor", ("batch", "context")),
            P(),
            P(),
            P(),
            P(("batch", "context"), "tensor"),
            P("tensor"),
            P("tensor", ("batch", "context")),
            P(),
        ),
        check_vma=False,
    )
```

profile of v0, /device:TPU:0, one launch (start us, length us, event | category | flops | bytes accessed | tf_op | source)
XLA Modules:
  0.0 1013.3 jit_solution(5012415796332199442)
XLA Ops:
  10.5 6.7 convolution_bitcast_fusion.1
  23.1 12.8 %all_gather.10 = bf16[1,1024]{1,0:T(2,128)(2,1)S(1)} all-gather(bf16[1,256]{1,0:T(2,128)(2,1)S(1)} %and_convert_fusion), channel_id=1, replica_groups=mesh['tensor'=2,'batch'=4,'context'=4] {'context'}, dimensions={1}, use_global_device_ids=true | all-gather | bytes 2560 | tf_op jit(solution)/shard_map/all_gather | solution.py:97
  36.3 32.1 %all-gather.4.cloned.1.call-done = bf16[1,1024,1024]{2,1,0:T(8,128)(2,1)} async-done(((bf16[1,256,1024]{2,1,0:T(8,128)(2,1)}), bf16[1,1024,1024]{2,1,0:T(8,128)(2,1)}) %all-gather.4.cloned.1.call-update) | async-done | bytes 2097168 | tf_op jit(solution)/shard_map/all_gather | solution.py:96
  71.9 43.1 %all-gather.6.cloned.1.call-done = bf16[1,1,1024,1024]{3,2,0,1:T(8,128)(2,1)} async-done(((bf16[1,1,256,1024]{3,2,0,1:T(8,128)(2,1)}), bf16[1,1,1024,1024]{3,2,0,1:T(8,128)(2,1)}) %all-gather.6.cloned.1.call-update) | async-done | bytes 2097168 | tf_op jit(solution)/shard_map/all_gather | solution.py:95
  131.7 38.5 %all-reduce.6.cloned.1.call-done = bf16[1,256,2048]{2,1,0:T(8,128)(2,1)} async-done(((bf16[1,256,2048]{2,1,0:T(8,128)(2,1)}), bf16[1,256,2048]{2,1,0:T(8,128)(2,1)}) %all-reduce.6.cloned.1.call-update) | async-done | bytes 1048592 | tf_op jit(solution)/shard_map/psum | solution.py:52
  172.6 8.5 convolution_add_fusion
  181.1 12.9 %fusion.79 = (bf16[4096]{0:T(1024)(128)(2,1)S(1)}, bf16[256,4096]{1,0:T(8,128)(2,1)}) fusion(f32[256,4096]{1,0:T(8,128)S(1)} %convolution_add_fusion, bf16[4096,2048]{1,0:T(8,128)(2,1)} %param.27, bf16[1,256,2048]{2,1,0:T(8,128)(2,1)S(1)} %copy-done.14, f32[256]{0:T(256)S(1)} %compare_convert_fusion), kind=kOutput, calls=%fused_computation.121 | convolution fusion | flops 4318556160 | bytes 24126464 | tf_op jit(solution)/shard_map/std,fd->stf/dot_general | solution.py:134
  194.0 11.9 %fusion.21 = bf16[1,256,2048]{2,1,0:T(8,128)(2,1)} fusion(bf16[256,4096]{1,0:T(8,128)(2,1)} %get-tuple-element.44, bf16[2048,4096]{1,0:T(8,128)(2,1)} %param.25), kind=kOutput, calls=%fused_computation.46 | convolution fusion | flops 4295491584 | bytes 19922944 | tf_op jit(solution)/shard_map/stf,df->std/dot_general | solution.py:142
  206.2 40.0 %all-reduce.8.cloned.1.call-done = bf16[1,256,2048]{2,1,0:T(8,128)(2,1)} async-done(((bf16[1,256,2048]{2,1,0:T(8,128)(2,1)}), bf16[1,256,2048]{2,1,0:T(8,128)(2,1)}) %all-reduce.8.cloned.1.call-update) | async-done | bytes 1048592 | tf_op jit(solution)/shard_map/psum | solution.py:52
  255.8 7.3 convolution_convert_fusion.7
  267.1 7.3 multiply_reduce_fusion
  286.0 13.2 %fusion.20 = bf16[1,256,2048]{2,1,0:T(8,128)(2,1)} fusion(bf16[4096,2048]{1,0:T(8,128)(2,1)} %param.27, f32[256,4096]{1,0:T(8,128)} %copy-done.29), kind=kOutput, calls=%fused_computation.45 | convolution fusion | flops 4304928768 | bytes 22020096 | tf_op jit(solution)/shard_map/stf,fd->std/dot_general | solution.py:124
  301.0 9.8 reduce-scatter.13.cloned.1.call-done
  310.8 45.0 %reduce-scatter.11.cloned.1.call-done = bf16[1,256,1024]{2,1,0:T(8,128)(2,1)} async-done(((bf16[1,1024,1024]{2,1,0:T(8,128)(2,1)}), bf16[1,256,1024]{2,1,0:T(8,128)(2,1)}) %reduce-scatter.11.cloned.1.call-update) | async-done | bytes 524304 | tf_op jit(solution)/shard_map/reduce_scatter | solution.py:179
  355.8 9.3 fusion.23
  371.1 6.4 copy.58
  378.5 7.7 convolution_convert_fusion.2
  387.5 11.7 %convolution_convert_fusion = bf16[4096,2048]{1,0:T(8,128)(2,1)} fusion(bf16[1,256,2048]{2,1,0:T(8,128)(2,1)S(1)} %copy-done.16, f32[256]{0:T(256)S(1)} %compare_convert_fusion, f32[256,4096]{1,0:T(8,128)} %copy-done.29), kind=kOutput, calls=%fused_computation | convolution fusion | flops 4314365952 | bytes 22021120 | tf_op jit(solution)/shard_map/stf,std->fd/dot_general | solution.py:130
  399.1 21.4 %copy.60 = bf16[4096,2048]{0,1:T(8,128)(2,1)} copy(bf16[4096,2048]{1,0:T(8,128)(2,1)} %convolution_convert_fusion) | data formatting | bytes 33554432
  420.6 9.9 convolution_convert_fusion.1
  436.8 60.5 %all-reduce = (bf16[2048]{0:T(1024)(128)(2,1)S(1)}, bf16[2048]{0:T(1024)(128)(2,1)S(1)}, bf16[2,1024]{1,0:T(2,128)(2,1)S(1)}, bf16[2048]{0:T(1024)(128)(2,1)S(1)...) all-reduce(bf16[2048]{0:T(1024)(128)(2,1)S(1)} %get-tuple-element.1, ...), channel_id=1, replica_groups=mesh['tensor'=2,'batch'=4,'context'=4] {'batch','context'}, use_global_device_ids=true, to_apply=%region_18.19 | all-reduce | flops 18432 | bytes 73728 | tf_op jit(solution)/shard_map/psum | solution.py:228
  508.7 133.7 %reduce-scatter.15.cloned.1.call-done = bf16[128,3,1024]{2,0,1:T(8,128)(2,1)} async-done(((bf16[2048,3,1024]{2,0,1:T(8,128)(2,1)}), bf16[128,3,1024]{2,0,1:T(8,128)(2,1)}) %reduce-scatter.15.cloned.1.call-update) | async-done | bytes 786448 | tf_op jit(solution)/shard_map/reduce_scatter | solution.py:212
  644.8 178.1 %reduce-scatter.21.cloned.1.call-done = bf16[128,4096]{1,0:T(8,128)(2,1)} async-done(((bf16[2048,4096]{1,0:T(8,128)(2,1)}), bf16[128,4096]{1,0:T(8,128)(2,1)}) %reduce-scatter.21.cloned.1.call-update) | async-done | bytes 1048592
  826.0 177.5 %reduce-scatter.17.cloned.1.call-done = bf16[128,4096]{1,0:T(8,128)(2,1)} async-done(((bf16[2048,4096]{1,0:T(8,128)(2,1)}), bf16[128,4096]{1,0:T(8,128)(2,1)}) %reduce-scatter.17.cloned.1.call-update) | async-done | bytes 1048592 | tf_op jit(solution)/shard_map/reduce_scatter | solution.py:215
  (146 shorter events, 92.6 us)
Async XLA Ops:
  7.2 3.3 copy-start.1
  7.2 61.1 %all-gather.4.cloned.1.call-start = ((), (), s32[]{:S(2)}) async-start(), calls=%async_computation.6 | async-start | bytes 2621440 | tf_op jit(solution)/shard_map/all_gather | solution.py:96
  19.8 95.2 %all-gather.6.cloned.1.call-start = ((), (), s32[]{:S(2)}) async-start(), calls=%async_computation.13 | async-start | bytes 2621440 | tf_op jit(solution)/shard_map/all_gather | solution.py:95
  22.0 148.2 %all-reduce.6.cloned.1.call-start = ((), (), s32[]{:S(2)}) async-start(), calls=%async_computation.7 | async-start | bytes 2097152 | tf_op jit(solution)/shard_map/psum | solution.py:52
  122.7 3.5 copy-start
  122.7 3.5 copy-start.10
  128.9 41.3 %copy-start.18 = (f32[2048]{0:T(1024)S(1)}, f32[2048]{0:T(1024)}, u32[]{:S(2)}) copy-start(f32[2048]{0:T(1024)} %param.22) | copy-start | bytes 24580
  131.2 115.0 %all-reduce.8.cloned.1.call-start = ((), (), s32[]{:S(2)}) async-start(), calls=%async_computation.8 | async-start | bytes 2097152 | tf_op jit(solution)/shard_map/psum | solution.py:52
  131.7 40.9 %copy-start.19 = (f32[2048]{0:T(1024)S(1)}, f32[2048]{0:T(1024)}, u32[]{:S(2)}) copy-start(f32[2048]{0:T(1024)} %param.23) | copy-start | bytes 24580
  131.7 40.9 %copy-start.21 = (f32[2048]{0:T(1024)S(1)}, f32[2048]{0:T(1024)}, u32[]{:S(2)}) copy-start(f32[2048]{0:T(1024)} %param.24) | copy-start | bytes 24580
  131.7 40.9 %copy-start.27 = (f32[4096]{0:T(1024)S(1)}, f32[4096]{0:T(1024)}, u32[]{:S(2)}) copy-start(f32[4096]{0:T(1024)} %param.26) | copy-start | bytes 49156
  172.6 8.5 copy-start.14
  181.1 12.9 %copy-start.29 = (f32[256,4096]{1,0:T(8,128)}, f32[256,4096]{1,0:T(8,128)S(1)}, u32[]{:S(2)}) copy-start(f32[256,4096]{1,0:T(8,128)S(1)} %convolution_add_fusion) | copy-start | bytes 12582916
  205.9 104.9 %reduce-scatter.13.cloned.1.call-start = ((), (), s32[]{:S(2)}) async-start(), calls=%async_computation.10 | async-start | bytes 2621440 | tf_op jit(solution)/shard_map/reduce_scatter | solution.py:185
  267.1 88.8 %reduce-scatter.11.cloned.1.call-start = ((), (), s32[]{:S(2)}) async-start(), calls=%async_computation.9 | async-start | bytes 2621440 | tf_op jit(solution)/shard_map/reduce_scatter | solution.py:179
  285.8 147.3 %all-reduce.10.cloned.1.call-start = ((), (), s32[]{:S(2)}) async-start(), calls=%async_computation.16 | async-start | bytes 4194304 | tf_op jit(solution)/shard_map/psum | solution.py:52
  286.0 13.2 %copy-start.4 = (bf16[8,256,1024]{2,1,0:T(8,128)(2,1)S(1)}, bf16[8,256,1024]{2,1,0:T(8,128)(2,1)}, u32[]{:S(2)}) copy-start(bf16[8,256,1024]{2,1,0:T(8,128)(2,1)} %copy-done.3) | copy-start | bytes 12582916
  286.0 13.2 %copy-start.6 = (bf16[1,1,1024,1024]{2,3,1,0:T(8,128)(2,1)S(1)}, bf16[1,1,1024,1024]{2,3,1,0:T(8,128)(2,1)}, u32[]{:S(2)}) copy-start(bf16[1,1,1024,1024]{2,3,1,0:T(8,128)(2,1)} %copy.62) | copy-start | bytes 6291460
  365.2 141.5 %reduce-scatter.19.cloned.1.call-start = ((), (), s32[]{:S(2)}) async-start(), calls=%async_computation.14 | async-start | bytes 4456448
  377.5 264.9 %reduce-scatter.15.cloned.1.call-start = ((), (), s32[]{:S(2)}) async-start(), calls=%async_computation.11 | async-start | bytes 13369344 | tf_op jit(solution)/shard_map/reduce_scatter | solution.py:212
  386.3 436.7 %reduce-scatter.21.cloned.1.call-start = ((), (), s32[]{:S(2)}) async-start(), calls=%async_computation.15 | async-start | bytes 17825792
  420.6 583.0 %reduce-scatter.17.cloned.1.call-start = ((), (), s32[]{:S(2)}) async-start(), calls=%async_computation.12 | async-start | bytes 17825792 | tf_op jit(solution)/shard_map/reduce_scatter | solution.py:215
  431.9 70.2 %copy-start.22 = (f32[2048]{0:T(1024)S(1)}, f32[2048]{0:T(1024)}, u32[]{:S(2)}) copy-start(f32[2048]{0:T(1024)} %param.28) | copy-start | bytes 24580
  433.1 69.0 %copy-start.7 = (bf16[1,256,2048]{2,1,0:T(8,128)(2,1)S(1)}, bf16[1,256,2048]{2,1,0:T(8,128)(2,1)}, u32[]{:S(2)}) copy-start(bf16[1,256,2048]{2,1,0:T(8,128)(2,1)} %get-tuple-element.29) | copy-start | bytes 3145732
  (18 other events, 38.8 us)
Sparse Core Ops, SparseCore 0:
  19.9 48.3 all-gather.3
  70.5 44.4 all-gather.5
  131.3 38.8 all-reduce.5
  206.1 40.0 all-reduce.7
  267.2 43.6 reduce-scatter.12
  313.0 42.8 reduce-scatter.10
  365.3 62.1 all-reduce.9
  431.4 73.0 reduce-scatter.18
  508.5 133.7 reduce-scatter.14
  646.3 176.5 reduce-scatter.20
  827.1 176.4 reduce-scatter.16
where the time goes:
time: 1020 us; the launch traced here: 1010 us
  waiting for transfers between devices  698 us (68%)
  matrix products  126 us (12%)
  blocking collectives  73.3 us (7%)
  local copies, waits for them, and re-layouts  59.1 us (6%)
  other arithmetic  39.6 us (4%)
  between operations  15.4 us (2%)
    unnamed x13, waiting for transfers between devices  178 us
    reduce_scatter x1, waiting for transfers between devices, local(): lax.psum_scatter(expand_grad.astype(jnp.bfloat16), ('batch', 'context'),...  177 us
    reduce_scatter x1, waiting for transfers between devices, local(): lax.psum_scatter(attend_grad.astype(jnp.bfloat16), ('batch', 'context'),...  134 us
    psum x3, waiting for transfers between devices, tensor_total(): return lax.psum(values.astype(jnp.bfloat16), 'tensor').astype(jnp.float32)  78.5 us
    psum x1, blocking collectives, local(): lax.psum(gain_one_grad.astype(jnp.bfloat16), ('batch', 'context'))  60.5 us
    reduce_scatter x1, waiting for transfers between devices, local(): lax.psum_scatter(key_part.reshape(seq_count, full_len, local_width).astyp...  45 us
    all_gather x1, waiting for transfers between devices, local(): lax.all_gather(keys_own, 'context', axis=1, tiled=True)  43.1 us
    unnamed x66, local copies, waits for them, and re-layouts  42.5 us
  transfers between devices with their start and end apart: 11, of which 9 were waited for; matrix products, arithmetic and copies ran while one was open for 12% of the time, Pallas kernels for 0%

commit v1 on v0

--- a/solution.py
+++ b/solution.py
@@ -1,6 +1,10 @@
+import functools
+
 import jax
 import jax.numpy as jnp
 from jax import lax
+from jax.experimental import pallas as pl
+from jax.experimental.pallas import tpu as pltpu
 from jax.sharding import PartitionSpec as P
 
 HEAD_DIM = 128
@@ -52,7 +56,7 @@
     return lax.psum(values.astype(jnp.bfloat16), "tensor").astype(jnp.float32)
 
 
-def local(
+def general(
     block_input,
     gain_first,
     shift_first,
@@ -250,6 +254,841 @@
         reduce_total,
         smalls[7],
     )
+
+
+MESH = pl.DeviceIdType.MESH
+F32 = jnp.float32
+BF16 = jnp.bfloat16
+VMEM_WHOLE = pl.BlockSpec(memory_space=pltpu.VMEM)
+TILE = 512
+
+
+def mm(left, right):
+    return lax.dot_general(left, right, (((1,), (0,)), ((), ())), preferred_element_type=F32)
+
+
+def mm_nt(left, right):
+    return lax.dot_general(left, right, (((1,), (1,)), ((), ())), preferred_element_type=F32)
+
+
+def mm_tn(left, right):
+    return lax.dot_general(left, right, (((0,), (0,)), ((), ())), preferred_element_type=F32)
+
+
+def whole(shape):
+    return pl.BlockSpec(shape, lambda *ids: (0,) * len(shape))
+
+
+def call(body, grid, ins, outs, operands, scratch=(), flops=0, moved=0, name=None):
+    in_specs = [spec for spec in ins]
+    return pl.pallas_call(
+        body,
+        grid_spec=pltpu.PrefetchScalarGridSpec(
+            num_scalar_prefetch=1,
+            grid=grid,
+            in_specs=in_specs,
+            out_specs=[spec for spec, _ in outs],
+            scratch_shapes=list(scratch),
+        ),
+        out_shape=[shape for _, shape in outs],
+        cost_estimate=pl.CostEstimate(flops=flops, bytes_accessed=moved, transcendentals=0),
+        name=name,
+    )(*operands)
+
+
+def sds(shape, kind):
+    return jax.ShapeDtypeStruct(shape, kind)
+
+
+def norm_rows(values):
+    average = jnp.mean(values, -1, keepdims=True)
+    center = values - average
+    inverse = lax.rsqrt(jnp.mean(center * center, -1, keepdims=True) + EPS)
+    return center * inverse, inverse
+
+
+def qkv_body(pos, x_ref, gain_ref, shift_ref, w_ref, off_ref, out_ref, normed_ref):
+    part = pl.program_id(0)
+
+    @pl.when((part == 0) & (pl.program_id(1) == 0))
+    def _():
+        normal, _ = norm_rows(x_ref[...].astype(F32))
+        normed_ref[...] = (normal * gain_ref[...] + shift_ref[...]).astype(BF16)
+
+    bias = jnp.where(part == 0, off_ref[0:1, :], jnp.where(part == 2, off_ref[1:2, :], 0.0))
+    out_ref[...] = (mm(normed_ref[...], w_ref[...]) + bias).astype(BF16)
+
+
+def qkv_call(pos, x, gain, shift, weight, offset):
+    rows, depth = x.shape
+    width = weight.shape[2]
+    return call(
+        qkv_body,
+        (3, width // TILE),
+        [
+            whole((rows, depth)),
+            whole((1, depth)),
+            whole((1, depth)),
+            pl.BlockSpec((None, depth, TILE), lambda c, n, pos: (c, 0, n)),
+            pl.BlockSpec((2, TILE), lambda c, n, pos: (0, n)),
+        ],
+        [
+            (pl.BlockSpec((None, rows, TILE), lambda c, n, pos: (c, 0, n)), sds((3, rows, width), BF16)),
+            (whole((rows, depth)), sds((rows, depth), BF16)),
+        ],
+        (pos, x, gain, shift, weight, offset),
+        flops=2 * rows * depth * 3 * width,
+        moved=2 * depth * 3 * width,
+        name="qkv",
+    )
+
+
+def greet(peers):
+    barrier = pltpu.get_barrier_semaphore()
+    for peer in peers:
+        pl.semaphore_signal(barrier, inc=1, device_id=peer, device_id_type=MESH)
+    pl.semaphore_wait(barrier, len(peers))
+
+
+def spread_body(n, parts, with_flags, *refs):
+    if with_flags:
+        src, flags, dst, all_flags, send, recv, fsend, frecv = refs
+    else:
+        src, dst, send, recv = refs
+    me = lax.axis_index("context")
+    rows = src.shape[1]
+    cols = src.shape[2] // n
+    greet([{"context": lax.rem(me + r, n)} for r in range(1, n)])
+    mine = pl.ds(pl.multiple_of(me * rows, rows), rows)
+    copies = []
+    for c in range(parts):
+        for r in range(1, n):
+            to = lax.rem(me + r, n)
+            copies.append(
+                pltpu.make_async_remote_copy(
+                    src_ref=src.at[c, :, pl.ds(pl.multiple_of(to * cols, cols), cols)],
+                    dst_ref=dst.at[c, mine, :],
+                    send_sem=send.at[c, r - 1],
+                    recv_sem=recv.at[c, r - 1],
+                    device_id={"context": to},
+                    device_id_type=MESH,
+                )
+            )
+    if with_flags:
+        for r in range(1, n):
+            copies.append(
+                pltpu.make_async_remote_copy(
+                    src_ref=flags,
+                    dst_ref=all_flags.at[me],
+                    send_sem=fsend.at[r - 1],
+                    recv_sem=frecv.at[r - 1],
+                    device_id={"context": lax.rem(me + r, n)},
+                    device_id_type=MESH,
+                )
+            )
+    for copy in copies:
+        copy.start()
+    for c in range(parts):
+        dst[c, mine, :] = src[c, :, pl.ds(pl.multiple_of(me * cols, cols), cols)]
+    if with_flags:
+        all_flags[me] = flags[...]
+    for copy in copies:
+        copy.wait()
+
+
+def spread(n, src, flags, collective):
+    parts, rows, width = src.shape
+    with_flags = flags is not None
+    outs = [sds((parts, n * rows, width // n), BF16)]
+    scratch = [pltpu.SemaphoreType.DMA((parts, n - 1))] * 2
+    if with_flags:
+        outs.append(sds((n, *flags.shape), flags.dtype))
+        scratch += [pltpu.SemaphoreType.DMA((n - 1,))] * 2
+    return pl.pallas_call(
+        functools.partial(spread_body, n, parts, with_flags),
+        out_shape=outs,
+        in_specs=[VMEM_WHOLE] * (1 + with_flags),
+        out_specs=[VMEM_WHOLE] * len(outs),
+        scratch_shapes=scratch,
+        compiler_params=pltpu.CompilerParams(collective_id=collective, has_side_effects=True),
+        name=f"spread{collective}",
+    )(*((src, flags) if with_flags else (src,)))
+
+
+def collect_body(n, parts, src, dst, send, recv):
+    me = lax.axis_index("context")
+    rows = src.shape[1] // n
+    cols = src.shape[2]
+    greet([{"context": lax.rem(me + r, n)} for r in range(1, n)])
+    mine = pl.ds(pl.multiple_of(me * cols, cols), cols)
+    copies = []
+    for c in range(parts):
+        for r in range(1, n):
+            to = lax.rem(me + r, n)
+            copies.append(
+                pltpu.make_async_remote_copy(
+                    src_ref=src.at[c, pl.ds(pl.multiple_of(to * rows, rows), rows), :],
+                    dst_ref=dst.at[c, :, mine],
+                    send_sem=send.at[c, r - 1],
+                    recv_sem=recv.at[c, r - 1],
+                    device_id={"context": to},
+                    device_id_type=MESH,
+                )
+            )
+    for copy in copies:
+        copy.start()
+    for c in range(parts):
+        dst[c, :, mine] = src[c, pl.ds(pl.multiple_of(me * rows, rows), rows), :]
+    for copy in copies:
+        copy.wait()
+
+
+def collect(n, src, collective):
+    parts, rows, width = src.shape
+    return pl.pallas_call(
+        functools.partial(collect_body, n, parts),
+        out_shape=sds((parts, rows // n, width * n), BF16),
+        in_specs=[VMEM_WHOLE],
+        out_specs=VMEM_WHOLE,
+        scratch_shapes=[pltpu.SemaphoreType.DMA((parts, n - 1))] * 2,
+        compiler_params=pltpu.CompilerParams(collective_id=collective, has_side_effects=True),
+        name=f"collect{collective}",
+    )(src)
+
+
+def mixed_body(n, src, dst, own, send, recv, xsend, xrecv):
+    me = lax.axis_index("context")
+    side = lax.axis_index("tensor")
+    rows = src.shape[0] // n
+    cols = src.shape[1]
+    width = n * cols
+    greet([{"context": lax.rem(me + r, n)} for r in range(1, n)] + [{"tensor": 1 - side}])
+
+    def place(origin):
+        return dst.at[:, pl.ds(pl.multiple_of(side * width + origin * cols, cols), cols)]
+
+    copies = []
+    for r in range(1, n):
+        to = lax.rem(me + r, n)
+        copies.append(
+            pltpu.make_async_remote_copy(
+                src_ref=src.at[pl.ds(pl.multiple_of(to * rows, rows), rows), :],
+                dst_ref=place(me),
+                send_sem=send.at[r - 1],
+                recv_sem=recv.at[r - 1],
+                device_id={"context": to},
+                device_id_type=MESH,
+            )
+        )
+    for copy in copies:
+        copy.start()
+    across = []
+    for r in range(n):
+        origin = lax.rem(me + n - r, n)
+        if r:
+            copies[r - 1].wait()
+            source = place(origin)
+        else:
+            source = src.at[pl.ds(pl.multiple_of(me * rows, rows), rows), :]
+        copy = pltpu.make_async_remote_copy(
+            src_ref=source,
+            dst_ref=place(origin),
+            send_sem=xsend.at[r],
+            recv_sem=xrecv.at[r],
+            device_id={"tensor": 1 - side},
+            device_id_type=MESH,
+        )
+        copy.start()
+        across.append(copy)
+        if not r:
+            here = pl.ds(pl.multiple_of(side * width + me * cols, cols), cols)
+            dst[:, here] = src[pl.ds(pl.multiple_of(me * rows, rows), rows), :]
+    own[...] = dst[:, pl.ds(pl.multiple_of(side * width, width), width)]
+    for copy in across:
+        copy.wait()
+
+
+def mixed_call(n, src, collective):
+    rows, cols = src.shape
+    return pl.pallas_call(
+        functools.partial(mixed_body, n),
+        out_shape=[sds((rows // n, 2 * n * cols), BF16), sds((rows // n, n * cols), BF16)],
+        in_specs=[VMEM_WHOLE],
+        out_specs=[VMEM_WHOLE] * 2,
+        scratch_shapes=[pltpu.SemaphoreType.DMA((n - 1,))] * 2 + [pltpu.SemaphoreType.DMA((n,))] * 2,
+        compiler_params=pltpu.CompilerParams(collective_id=collective, has_side_effects=True),
+        name="mixed_exchange",
+    )(src)
+
+
+def allowed_block(row, size, count, flags):
+    query = row * size + lax.broadcasted_iota(jnp.int32, (size, count), 0)
+    key = lax.broadcasted_iota(jnp.int32, (size, count), 1)
+    return (key <= query) & ((flags[:, :count] > 0.5) | (key == query))
+
+
+def key_row(flag_ref):
+    return jnp.concatenate([flag_ref[j, 0:1, :] for j in range(flag_ref.shape[0])], axis=1)
+
+
+def attend_body(n, pos, qkv_ref, flag_ref, mixed_ref, lse_ref):
+    size = qkv_ref.shape[1] // n
+    scale = HEAD_DIM ** (-0.5)
+    flags = key_row(flag_ref)
+    for row in range(n):
+        count = size * (row + 1)
+        rows = slice(row * size, count)
+        scores = mm_nt(qkv_ref[0, rows, :], qkv_ref[1, :count, :]) * scale
+        scores = jnp.where(allowed_block(row, size, count, flags), scores, NEGATIVE)
+        top = jnp.max(scores, -1, keepdims=True)
+        total = top + jnp.log(jnp.sum(jnp.exp(scores - top), -1, keepdims=True))
+        weights = jnp.exp(scores - total).astype(BF16)
+        mixed_ref[rows, :] = mm(weights, qkv_ref[2, :count, :]).astype(BF16)
+        lse_ref[rows, :] = jnp.broadcast_to(total, (size, HEAD_DIM))
+
+
+def attend_call(n, pos, qkv, flags):
+    _, full, width = qkv.shape
+    heads = width // HEAD_DIM
+    return call(
+        functools.partial(attend_body, n),
+        (heads,),
+        [pl.BlockSpec((3, full, HEAD_DIM), lambda h, pos: (0, 0, h)), whole(flags.shape)],
+        [
+            (pl.BlockSpec((full, HEAD_DIM), lambda h, pos: (0, h)), sds((full, width), BF16)),
+            (pl.BlockSpec((full, HEAD_DIM), lambda h, pos: (0, h)), sds((full, width), F32)),
+        ],
+        (pos, qkv, flags),
+        flops=4 * full * full * width,
+        moved=10 * full * width,
+        name="attend",
+    )
+
+
+def attend_back_body(n, pos, qkv_ref, flag_ref, lse_ref, up_ref, out_ref, dk_ref, dv_ref):
+    size = qkv_ref.shape[1] // n
+    scale = HEAD_DIM ** (-0.5)
+    flags = key_row(flag_ref)
+    dk_ref[...] = jnp.zeros_like(dk_ref)
+    dv_ref[...] = jnp.zeros_like(dv_ref)
+    for row in range(n):
+        count = size * (row + 1)
+        rows = slice(row * size, count)
+        query = qkv_ref[0, rows, :]
+        up = up_ref[rows, :]
+        scores = mm_nt(query, qkv_ref[1, :count, :]) * scale
+        scores = jnp.where(allowed_block(row, size, count, flags), scores, NEGATIVE)
+        weights = jnp.exp(scores - lse_ref[rows, 0:1])
+        weights_grad = mm_nt(up, qkv_ref[2, :count, :])
+        row_dot = jnp.sum(weights * weights_grad, -1, keepdims=True)
+        score_grad = (weights * (weights_grad - row_dot)).astype(BF16)
+        dv_ref[:count, :] += mm_tn(weights.astype(BF16), up)
+        dk_ref[:count, :] += mm_tn(score_grad, query)
+        out_ref[0, rows, :] = (mm(score_grad, qkv_ref[1, :count, :]) * scale).astype(BF16)
+    out_ref[1] = (dk_ref[...] * scale).astype(BF16)
+    out_ref[2] = dv_ref[...].astype(BF16)
+
+
+def attend_back_call(n, pos, qkv, flags, lse, up):
+    _, full, width = qkv.shape
+    heads = width // HEAD_DIM
+    return call(
+        functools.partial(attend_back_body, n),
+        (heads,),
+        [
+            pl.BlockSpec((3, full, HEAD_DIM), lambda h, pos: (0, 0, h)),
+            whole(flags.shape),
+            pl.BlockSpec((full, HEAD_DIM), lambda h, pos: (0, h)),
+            pl.BlockSpec((full, HEAD_DIM), lambda h, pos: (0, h)),
+        ],
+        [(pl.BlockSpec((3, full, HEAD_DIM), lambda h, pos: (0, 0, h)), sds((3, full, width), BF16))],
+        (pos, qkv, flags, lse, up),
+        scratch=[pltpu.VMEM((full, HEAD_DIM), F32)] * 2,
+        flops=10 * full * full * width,
+        moved=20 * full * width,
+        name="attend_back",
+    )[0]
+
+
+def merge_body(pos, x_ref, mixed_ref, own_ref, near_ref, far_ref, off_ref, gain_ref, shift_ref, middle_ref, normed_ref):
+    step = pl.program_id(0)
+    side, core = pos[0], lax.rem(pos[1], 2)
+    half = near_ref.shape[0]
+    tile = off_ref.shape[1]
+
+    def piece(which, part, weight):
+        start = pl.multiple_of(which * 2 * half + part * half, half)
+        return mm(mixed_ref[:, pl.ds(start, half)], weight)
+
+    own = piece(side, 0, own_ref[:half, :]) + piece(side, 1, own_ref[half:, :])
+    other = piece(1 - side, core, near_ref[...]) + piece(1 - side, 1 - core, far_ref[...])
+    columns = pl.ds(pl.multiple_of(step * tile, tile), tile)
+    middle_ref[:, columns] = x_ref[...].astype(F32) + (own + other) + off_ref[...]
+
+    @pl.when(step == pl.num_programs(0) - 1)
+    def _():
+        normal, _ = norm_rows(middle_ref[...])
+        normed_ref[...] = (normal * gain_ref[...] + shift_ref[...]).astype(BF16)
+
+
+def merge_call(pos, x, mixed, own, near, far, offset, gain, shift):
+    rows, depth = x.shape
+    half = near.shape[0]
+    column = lambda n, pos: (0, n)
+    return call(
+        merge_body,
+        (depth // TILE,),
+        [
+            pl.BlockSpec((rows, TILE), column),
+            whole(mixed.shape),
+            pl.BlockSpec((2 * half, TILE), column),
+            pl.BlockSpec((half, TILE), column),
+            pl.BlockSpec((half, TILE), column),
+            pl.BlockSpec((1, TILE), column),
+            whole((1, depth)),
+            whole((1, depth)),
+        ],
+        [(whole((rows, depth)), sds((rows, depth), F32)), (whole((rows, depth)), sds((rows, depth), BF16))],
+        (pos, x, mixed, own, near, far, offset, gain, shift),
+        flops=2 * rows * depth * 4 * half,
+        moved=8 * half * depth,
+        name="merge",
+    )
+
+
+GELU_SCALE = 0.7978845608028654
+GELU_CUBE = 0.044715
+
+
+def expand_body(pos, normed_ref, w_ref, off_ref, up_ref, r_ref, active_ref, grad_ref, sum_ref):
+    hidden = mm(normed_ref[...], w_ref[...]) + off_ref[...]
+    square = hidden * hidden
+    bend = jnp.tanh(GELU_SCALE * (hidden + GELU_CUBE * (square * hidden)))
+    half = 0.5 * (1.0 + bend)
+    active_ref[...] = (hidden * half).astype(BF16)
+    slope = half + (0.5 * GELU_SCALE) * hidden * (1.0 - bend * bend) * (1.0 + (3.0 * GELU_CUBE) * square)
+    grad = (mm_nt(up_ref[...], r_ref[...]) * slope).astype(BF16)
+    grad_ref[...] = grad
+    sum_ref[...] = jnp.sum(grad.astype(F32), 0, keepdims=True)
+
+
+def expand_call(pos, part, parts, normed, weight, offset, up, reduce_weight):
+    rows, depth = normed.shape
+    width = weight.shape[1] // parts
+    base = part * (width // TILE)
+    return call(
+        expand_body,
+        (width // TILE,),
+        [
+            whole((rows, depth)),
+            pl.BlockSpec((depth, TILE), lambda n, pos: (0, base + n)),
+            pl.BlockSpec((1, TILE), lambda n, pos: (0, base + n)),
+            whole((rows, depth)),
+            pl.BlockSpec((TILE, depth), lambda n, pos: (base + n, 0)),
+        ],
+        [
+            (pl.BlockSpec((rows, TILE), lambda n, pos: (0, n)), sds((rows, width), BF16)),
+            (pl.BlockSpec((rows, TILE), lambda n, pos: (0, n)), sds((rows, width), BF16)),
+            (pl.BlockSpec((1, TILE), lambda n, pos: (0, n)), sds((1, width), F32)),
+        ],
+        (pos, normed, weight, offset, up, reduce_weight),
+        flops=4 * rows * depth * width,
+        moved=4 * depth * width,
+        name=f"expand{part}",
+    )
+
+
+def rows_body(count, pos, *refs):
+    w_ref, out_ref = refs[count], refs[count + 1]
+    start, total = 0, None
+    for ref in refs[:count]:
+        width = ref.shape[1]
+        term = mm_nt(ref[...], w_ref[:, start : start + width])
+        total = term if total is None else total + term
+        start += width
+    out_ref[...] = total.astype(BF16)
+
+
+def rows_call(pos, pieces, weight, name):
+    rows = pieces[0].shape[0]
+    depth, width = weight.shape
+    return call(
+        functools.partial(rows_body, len(pieces)),
+        (depth // TILE,),
+        [whole(piece.shape) for piece in pieces] + [pl.BlockSpec((TILE, width), lambda n, pos: (n, 0))],
+        [(pl.BlockSpec((rows, TILE), lambda n, pos: (0, n)), sds((rows, depth), BF16))],
+        (pos, *pieces, weight),
+        flops=2 * rows * depth * width,
+        moved=2 * depth * width,
+        name=name,
+    )[0]
+
+
+def columns_body(count, pos, *refs):
+    w_ref, out_ref = refs[count], refs[count + 1]
+    start, total = 0, None
+    for ref in refs[:count]:
+        width = ref.shape[1]
+        term = mm(ref[...], w_ref[start : start + width, :])
+        total = term if total is None else total + term
+        start += width
+    out_ref[...] = total.astype(BF16)
+
+
+def columns_call(pos, pieces, weight, name):
+    rows = pieces[0].shape[0]
+    width, depth = weight.shape
+    return call(
+        functools.partial(columns_body, len(pieces)),
+        (depth // TILE,),
+        [whole(piece.shape) for piece in pieces] + [pl.BlockSpec((width, TILE), lambda n, pos: (0, n))],
+        [(pl.BlockSpec((rows, TILE), lambda n, pos: (0, n)), sds((rows, depth), BF16))],
+        (pos, *pieces, weight),
+        flops=2 * rows * depth * width,
+        moved=2 * depth * width,
+        name=name,
+    )[0]
+
+
+def norm_back_rows(upstream, values, gain):
+    normal, inverse = norm_rows(values)
+    gain_part = jnp.sum(upstream * normal, 0, keepdims=True)
+    shift_part = jnp.sum(upstream, 0, keepdims=True)
+    scaled = upstream * gain
+    inner = scaled - jnp.mean(scaled, -1, keepdims=True) - normal * jnp.mean(scaled * normal, -1, keepdims=True)
+    return inverse * inner, gain_part, shift_part
+
+
+def middle_back_body(pos, own_ref, peer_ref, middle_ref, gain_ref, up_ref, w_ref, out_ref, grad_ref, low_ref, gg_ref, sg_ref, mg_ref):
+    @pl.when(pl.program_id(0) == 0)
+    def _():
+        upstream = own_ref[...].astype(F32) + peer_ref[...].astype(F32)
+        part, gg_ref[...], sg_ref[...] = norm_back_rows(upstream, middle_ref[...], gain_ref[...])
+        grad = up_ref[...].astype(F32) + part
+        grad_ref[...] = grad
+        low_ref[...] = grad.astype(BF16)
+        mg_ref[...] = jnp.sum(grad, 0, keepdims=True)
+
+    out_ref[...] = mm_nt(low_ref[...], w_ref[...]).astype(BF16)
+
+
+def middle_back_call(pos, own, peer, middle, gain, up, weight):
+    rows, depth = own.shape
+    width = weight.shape[0]
+    tile = TILE // 2
+    full, line = whole((rows, depth)), whole((1, depth))
+    return call(
+        middle_back_body,
+        (width // tile,),
+        [full, full, full, line, full, pl.BlockSpec((tile, depth), lambda n, pos: (n, 0))],
+        [
+            (pl.BlockSpec((rows, tile), lambda n, pos: (0, n)), sds((rows, width), BF16)),
+            (full, sds((rows, depth), F32)),
+            (full, sds((rows, depth), BF16)),
+            (line, sds((1, depth), F32)),
+            (line, sds((1, depth), F32)),
+            (line, sds((1, depth), F32)),
+        ],
+        (pos, own, peer, middle, gain, up, weight),
+        flops=2 * rows * depth * width,
+        moved=2 * depth * width,
+        name="middle_back",
+    )
+
+
+def first_body(pos, grads_ref, w_ref, out_ref, sum_ref):
+    @pl.when(pl.program_id(0) == 0)
+    def _():
+        sum_ref[0:1, :] = jnp.sum(grads_ref[0].astype(F32), 0, keepdims=True)
+        sum_ref[1:2, :] = jnp.sum(grads_ref[2].astype(F32), 0, keepdims=True)
+
+    total = mm_nt(grads_ref[0], w_ref[0]) + mm_nt(grads_ref[1], w_ref[1]) + mm_nt(grads_ref[2], w_ref[2])
+    out_ref[...] = total.astype(BF16)
+
+
+def first_call(pos, grads, weight):
+    _, rows, width = grads.shape
+    depth = weight.shape[1]
+    return call(
+        first_body,
+        (depth // TILE,),
+        [whole(grads.shape), pl.BlockSpec((3, TILE, width), lambda n, pos: (0, n, 0))],
+        [
+            (pl.BlockSpec((rows, TILE), lambda n, pos: (0, n)), sds((rows, depth), BF16)),
+            (whole((2, width)), sds((2, width), F32)),
+        ],
+        (pos, grads, weight),
+        flops=6 * rows * depth * width,
+        moved=6 * depth * width,
+        name="first_part",
+    )
+
+
+def input_back_body(own_ref, peer_ref, x_ref, gain_ref, grad_ref, out_ref, gg_ref, sg_ref):
+    upstream = own_ref[...].astype(F32) + peer_ref[...].astype(F32)
+    part, gg_ref[...], sg_ref[...] = norm_back_rows(upstream, x_ref[...].astype(F32), gain_ref[...])
+    out_ref[...] = (grad_ref[...] + part).astype(BF16)
+
+
+def input_back_call(own, peer, x, gain, grad):
+    rows, depth = own.shape
+    return pl.pallas_call(
+        input_back_body,
+        out_shape=[sds((rows, depth), BF16), sds((1, depth), F32), sds((1, depth), F32)],
+        name="input_back",
+    )(own, peer, x, gain, grad)
+
+
+def weight_body(pos, *refs):
+    out_ref = refs[-1]
+    total = None
+    for d_ref, t_ref in zip(refs[:4], refs[4:8]):
+        term = mm_tn(d_ref[...], t_ref[...])
+        total = term if total is None else total + term
+    out_ref[...] = total.astype(BF16)
+
+
+def weight_call(pos, sides, pieces, name):
+    rows, depth = sides[0].shape
+    quarter = depth // 4
+    width = pieces[0].shape[1]
+    return call(
+        weight_body,
+        (width // TILE,),
+        [
+            pl.BlockSpec((rows, quarter), lambda n, pos: (0, pos[1])),
+            pl.BlockSpec((rows, quarter), lambda n, pos: (0, lax.rem(pos[1], 2))),
+            whole((rows, quarter)),
+            whole((rows, quarter)),
+        ]
+        + [pl.BlockSpec((rows, TILE), lambda n, pos: (0, n))] * 4,
+        [(pl.BlockSpec((quarter, TILE), lambda n, pos: (0, n)), sds((quarter, width), BF16))],
+        (pos, *sides, *pieces),
+        flops=8 * rows * quarter * width,
+        moved=8 * rows * width,
+        name=name,
+    )[0]
+
+
+def total_body(groups, src, out, here, there, send, recv):
+    axes = [name for name, _ in groups]
+    index = {name: lax.axis_index(name) for name in axes}
+    greet([{name: lax.rem(index[name] + r, n)} for name, n in groups for r in range(1, n)])
+    base = 0
+    for stage, ((name, n), slots) in enumerate(zip(groups, (here, there))):
+        me = index[name]
+        value = src[...] if stage == 0 else out[...]
+        slots[me] = value
+        copies = []
+        for r in range(1, n):
+            copies.append(
+                pltpu.make_async_remote_copy(
+                    src_ref=src if stage == 0 else out,
+                    dst_ref=slots.at[me],
+                    send_sem=send.at[base + r - 1],
+                    recv_sem=recv.at[base + r - 1],
+                    device_id={name: lax.rem(me + r, n)},
+                    device_id_type=MESH,
+                )
+            )
+        for copy in copies:
+            copy.start()
+        for copy in copies:
+            copy.wait()
+        base += n - 1
+        total = slots[0]
+        for i in range(1, n):
+            total = total + slots[i]
+        out[...] = total
+
+
+def total_call(groups, values, collective):
+    count = sum(n - 1 for _, n in groups)
+    return pl.pallas_call(
+        functools.partial(total_body, groups),
+        out_shape=sds(values.shape, F32),
+        in_specs=[VMEM_WHOLE],
+        out_specs=VMEM_WHOLE,
+        scratch_shapes=[pltpu.VMEM((n, *values.shape), F32) for _, n in groups]
+        + [pltpu.SemaphoreType.DMA((count,))] * 2,
+        compiler_params=pltpu.CompilerParams(collective_id=collective, has_side_effects=True),
+        name="totals",
+    )(values)
+
+
+def swap(values, axis, bit, size):
+    return lax.ppermute(values, axis, [(i, i ^ bit) for i in range(size)])
+
+
+def quick(
+    block_input,
+    gain_first,
+    shift_first,
+    attend_weight,
+    attend_offset,
+    merge_weight,
+    merge_offset,
+    gain_second,
+    shift_second,
+    expand_weight,
+    expand_offset,
+    reduce_weight,
+    reduce_offset,
+    key_mask,
+    true_lengths,
+    output_cotangent,
+):
+    rows, depth = block_input.shape[1:]
+    width = merge_weight.shape[0]
+    hidden_width = expand_weight.shape[1]
+    n = lax.axis_size("context")
+    side, batch, place = (lax.axis_index(name) for name in ("tensor", "batch", "context"))
+    pos = jnp.stack([side, batch, place]).astype(jnp.int32)
+    core, high = lax.rem(batch, 2), batch // 2
+
+    def line(values):
+        return values.reshape(1, -1)
+
+    def across(values):
+        return swap(values, "tensor", 1, 2)
+
+    def over_y(values):
+        return swap(values, "batch", 2, 4)
+
+    def over_core(values):
+        return swap(values, "batch", 1, 4)
+
+    def share_sides(values):
+        half, quarter = depth // 2, depth // 4
+        far = over_y(lax.dynamic_slice(values, (0, (1 - high) * half), (rows, half)))
+        near = over_core(lax.dynamic_slice(values, (0, (batch + 1 - 2 * core) * quarter), (rows, quarter)))
+        both = over_core(lax.dynamic_slice(far, (0, (1 - core) * quarter), (rows, quarter)))
+        return values, far, near, both
+
+    def share_pieces(values):
+        far = over_y(values)
+        return values, far, over_core(values), over_core(far)
+
+    x = block_input[0]
+    half_rows = width // 2
+    near_rows = across(lax.dynamic_slice(merge_weight, (core * half_rows, 0), (half_rows, depth)))
+    far_rows = over_core(near_rows)
+
+    position = place * rows + jnp.arange(rows, dtype=jnp.int32)
+    live = position < true_lengths[0]
+    up = jnp.where(live[:, None], output_cotangent[0], jnp.zeros_like(output_cotangent[0]))
+    reduce_off_grad = jnp.sum(up.astype(F32), 0)
+    flags = jnp.broadcast_to(((key_mask[0] == 1) & live).astype(F32)[None, :], (8, rows))
+
+    weight_three = jnp.transpose(attend_weight, (1, 0, 2))
+    qkv, normed = qkv_call(pos, x, line(gain_first), line(shift_first), weight_three, attend_offset)
+    heads, all_flags = spread(n, qkv, flags, 1)
+    mixed_heads, lse = attend_call(n, pos, heads, all_flags)
+    mixed_full, mixed = mixed_call(n, mixed_heads, 2)
+    middle, normed_two = merge_call(
+        pos, x, mixed_full, merge_weight, near_rows, far_rows, line(merge_offset), line(gain_second), line(shift_second)
+    )
+    up_sides = share_sides(up)
+    normed_sides = share_sides(normed)
+    mixed_pieces = share_pieces(mixed)
+    normed_two_sides = share_sides(normed_two)
+
+    parts = 2
+    actives, hidden_grads, hidden_sums = zip(
+        *[
+            expand_call(pos, k, parts, normed_two, expand_weight, line(expand_offset), up, reduce_weight)
+            for k in range(parts)
+        ]
+    )
+    active_pieces = [share_pieces(values) for values in actives]
+    hidden_pieces = [share_pieces(values) for values in hidden_grads]
+
+    second_own = rows_call(pos, hidden_grads, expand_weight, "second_part")
+    second_peer = across(second_own)
+    reduced_own = columns_call(pos, actives, reduce_weight, "reduced_part")
+    reduced_peer = across(reduced_own)
+    block_output = (
+        middle + (reduced_own.astype(F32) + reduced_peer.astype(F32)) + reduce_offset
+    ).astype(BF16)
+
+    mixed_grad, middle_grad, middle_low, gain_two_grad, shift_two_grad, merge_off_grad = middle_back_call(
+        pos, second_own, second_peer, middle, line(gain_second), up, merge_weight
+    )
+    mixed_grad_heads = spread(n, mixed_grad[None], None, 3)[0]
+    triple_heads = attend_back_call(n, pos, heads, all_flags, lse, mixed_grad_heads[0])
+    triple = collect(n, triple_heads, 4)
+    first_own, offset_grad = first_call(pos, triple, weight_three)
+    first_peer = across(first_own)
+    input_gradient, gain_one_grad, shift_one_grad = input_back_call(
+        first_own, first_peer, x, line(gain_first), middle_grad
+    )
+
+    def scatter(values, axis=0):
+        return lax.psum_scatter(values, "context", scatter_dimension=axis, tiled=True)
+
+    reduce_total = jnp.concatenate(
+        [
+            scatter(weight_call(pos, up_sides, pieces, f"reduce_grad{k}")).T.astype(F32)
+            for k, pieces in enumerate(active_pieces)
+        ],
+        axis=0,
+    )
+    expand_total = jnp.concatenate(
+        [
+            scatter(weight_call(pos, normed_two_sides, pieces, f"expand_grad{k}")).astype(F32)
+            for k, pieces in enumerate(hidden_pieces)
+        ],
+        axis=1,
+    )
+    middle_sides = share_sides(middle_low)
+    merge_total = scatter(weight_call(pos, middle_sides, mixed_pieces, "merge_grad")).T.astype(F32)
+    attend_total = jnp.stack(
+        [
+            scatter(weight_call(pos, normed_sides, share_pieces(triple[c]), f"attend_grad{c}")).astype(F32)
+            for c in range(3)
+        ],
+        axis=1,
+    )
+
+    smalls = [
+        gain_one_grad,
+        shift_one_grad,
+        offset_grad,
+        merge_off_grad,
+        gain_two_grad,
+        shift_two_grad,
+        *hidden_sums,
+        reduce_off_grad,
+    ]
+    flat = jnp.concatenate([values.reshape(-1) for values in smalls]).reshape(-1, 128)
+    totals = total_call((("batch", 4), ("context", n)), flat, 5).reshape(-1)
+    sizes = [depth, depth, 2 * width, depth, depth, depth, hidden_width, depth]
+    starts = [sum(sizes[:i]) for i in range(len(sizes))]
+    gain_one, shift_one, offset, merge_off, gain_two, shift_two, expand_off, reduce_off = (
+        totals[start : start + size] for start, size in zip(starts, sizes)
+    )
+    return (
+        block_output[None],
+        input_gradient[None],
+        gain_one,
+        shift_one,
+        attend_total,
+        offset.reshape(2, width),
+        merge_total,
+        merge_off,
+        gain_two,
+        shift_two,
+        expand_total,
+        expand_off,
+        reduce_total,
+        reduce_off,
+    )
+
+
+def local(*operands):
+    heads = operands[3].shape[2] // HEAD_DIM
+    fits = lax.axis_size("tensor") == 2 and lax.axis_size("batch") == 4 and heads % lax.axis_size("context") == 0
+    return (quick if fits else general)(*operands)
 
 
 def solution(mesh):

time: 1020 us -> 662 us (0.65)
  waiting for transfers between devices: 698 us -> 279 us
  Pallas kernels: 0 us -> 302 us
  matrix products: 126 us -> 0 us
  blocking collectives: 73.3 us -> 0 us
  local copies, waits for them, and re-layouts: 59.1 us -> 24 us
  other arithmetic: 39.6 us -> 12.1 us
  starting transfers between devices: 1.56 us -> 28 us
    reduce_scatter x4 -> x8, waiting for transfers between devices: 366 us -> 0.01 us  [scatter(): lax.psum_scatter(values, 'context', scatter_dimension=axis, tiled=True)]
    pallas_call x0 -> x24, Pallas kernels: none -> 302 us  [the longest x18 145 us: call(): pl.pallas_call(body, grid_spec=pltpu.PrefetchScalarGridSpec(num_scalar_pr...]
    ppermute x0 -> x41, waiting for transfers between devices: none -> 279 us  [swap(): return lax.ppermute(values, axis, [(i, i ^ bit) for i in range(size)])]
    unnamed x13 -> x8, waiting for transfers between devices: 178 us -> 0.13 us
    dot_general x18 -> x0, matrix products: 126 us -> none  [the longest x1 13.2 us: local(): jnp.einsum('stf,fd->std', active_low, reduce_weight, preferred_element_ty...]
    psum x3 -> x0, waiting for transfers between devices: 78.5 us -> none  [tensor_total(): return lax.psum(values.astype(jnp.bfloat16), 'tensor').astype(jnp.float32)]
    all_gather x2 -> x0, waiting for transfers between devices: 75.2 us -> none  [the longest x1 43.1 us: local(): lax.all_gather(keys_own, 'context', axis=1, tiled=True)]
    psum x1 -> x0, blocking collectives: 60.5 us -> none  [local(): lax.psum(gain_one_grad.astype(jnp.bfloat16), ('batch', 'context'))]
  transfers between devices with their start and end apart: 11 -> 49, of which waited for: 9 -> 22; matrix products, arithmetic and copies ran while one was open for 12% -> 3% of each run, Pallas kernels for 0% -> 39%
where the time goes in v1:
time: 662 us; the launch traced here: 660 us
  Pallas kernels  302 us (46%)
  waiting for transfers between devices  279 us (42%)
  starting transfers between devices  28 us (4%)
  local copies, waits for them, and re-layouts  24 us (4%)
  between operations  15.4 us (2%)
  other arithmetic  12.1 us (2%)
    ppermute x41, waiting for transfers between devices, swap(): return lax.ppermute(values, axis, [(i, i ^ bit) for i in range(size)])  279 us
    pallas_call x18, Pallas kernels, call(): pl.pallas_call(body, grid_spec=pltpu.PrefetchScalarGridSpec(num_scalar_pr...  145 us
    pallas_call x2, Pallas kernels, spread(): pl.pallas_call(functools.partial(spread_body, n, parts, with_flags), out_...  67.4 us
    pallas_call x1, Pallas kernels, collect(): pl.pallas_call(functools.partial(collect_body, n, parts), out_shape=sds((...  46 us
    ppermute x41, starting transfers between devices, swap(): return lax.ppermute(values, axis, [(i, i ^ bit) for i in range(size)])  27.3 us
    pallas_call x1, Pallas kernels, mixed_call(): pl.pallas_call(functools.partial(mixed_body, n), out_shape=[sds((rows //...  21.3 us
    pallas_call x1, Pallas kernels, total_call(): pl.pallas_call(functools.partial(total_body, groups), out_shape=sds(value...  16.8 us
    unnamed x114, local copies, waits for them, and re-layouts  13.7 us
  transfers between devices with their start and end apart: 49, of which 22 were waited for; matrix products, arithmetic and copies ran while one was open for 3% of the time, Pallas kernels for 39%

profile of v1, /device:TPU:0, one launch (start us, length us, event | category | flops | bytes accessed | tf_op | source)
XLA Modules:
  0.0 660.0 jit_solution(18178309036756217362)
XLA Ops:
  12.0 45.6 %collective-permute-done.near_ref = bf16[512,2048]{1,0:T(8,128)(2,1)S(1)} collective-permute-done((bf16[512,2048]{1,0:T(8,128)(2,1)S(1)}, bf16[512,2048]{1,0:T(8,128)(2,1)S(1)}, u32[]{:S(2)}, u32[]{:S(2)}) %collective-permute-start) | collective-permute-done | bytes 2097184 | tf_op jit(solution)/shard_map/ppermute | solution.py:920
  58.9 10.6 %qkv.1 = (bf16[3,256,1024]{2,1,0:T(8,128)(2,1)}, bf16[256,2048]{1,0:T(8,128)(2,1)}) custom-call(s32[3]{0:T(128)} %pad_add_fusion.pos, bf16[256,2048]{1,0:T(8,128)(2,1)} %bitcast.61, f32[1,2048]{1,0:T(1,128)} %bitcast.73, f32[1,2048]{1,0:T(1,128)} %bitcast.77, bf16[3,2048,1024]{2,1,0:T(8,128)(2,1)} %bitcast.59, f32[2,1024]{1,0:T(2,128)} %off_ref.1), custom_call_target="tpu_custom_call" | custom-call | flops 3221225472 | bytes 12582912 | tf_op jit(solution)/shard_map/qkv/pallas_call | solution.py:284
  70.2 42.5 %spread1.1 = (bf16[3,1024,256]{2,1,0:T(8,128)(2,1)}, f32[4,8,256]{2,1,0:T(8,128)}) custom-call(bf16[3,256,1024]{2,1,0:T(8,128)(2,1)} %get-tuple-element.41.refs_0_, f32[8,256]{1,0:T(8,128)} %broadcast_in_dim.35.refs_1_), custom_call_target="tpu_custom_call" | custom-call | tf_op jit(solution)/shard_map/spread1/pallas_call | solution.py:407
  120.0 21.3 %mixed_exchange.1 = (bf16[256,2048]{1,0:T(8,128)(2,1)}, bf16[256,1024]{1,0:T(8,128)(2,1)}) custom-call(bf16[1024,256]{1,0:T(8,128)(2,1)} %get-tuple-element.44.src), custom_call_target="tpu_custom_call" | custom-call | tf_op jit(solution)/shard_map/mixed_exchange/pallas_call | solution.py:513
  152.2 10.8 %expand0.1 = (bf16[256,2048]{1,0:T(8,128)(2,1)}, bf16[256,2048]{1,0:T(8,128)(2,1)}, f32[1,2048]{1,0:T(1,128)}) custom-call(s32[3]{0:T(128)} %pad_add_fusion.pos, bf16[256,2048]{1,0:T(8,128)(2,1)} %get-tuple-element.47.normed_ref.refs_0_, bf16[2048,4096]{1,0:T(8,128)(2,1)} %refs_2_.3, f32[1,4096]{1,0:T(1,128)} %bitcast.71, ...), custom_call_target="tpu_custom_call" | custom-call | flops 4294967296 | bytes 16777216 | tf_op jit(solution)/shard_map/expand0/pallas_call | solution.py:284
  163.0 10.9 %expand1.1 = (bf16[256,2048]{1,0:T(8,128)(2,1)}, bf16[256,2048]{1,0:T(8,128)(2,1)}, f32[1,2048]{1,0:T(1,128)}) custom-call(s32[3]{0:T(128)} %pad_add_fusion.pos, bf16[256,2048]{1,0:T(8,128)(2,1)} %get-tuple-element.47.normed_ref.refs_0_, bf16[2048,4096]{1,0:T(8,128)(2,1)} %refs_2_.3, f32[1,4096]{1,0:T(1,128)} %bitcast.72, ...), custom_call_target="tpu_custom_call" | custom-call | flops 4294967296 | bytes 16777216 | tf_op jit(solution)/shard_map/expand1/pallas_call | solution.py:284
  173.9 10.8 %second_part.1.own_ref = bf16[256,2048]{1,0:T(8,128)(2,1)} custom-call(s32[3]{0:T(128)} %pad_add_fusion.pos, bf16[256,2048]{1,0:T(8,128)(2,1)} %get-tuple-element.51.refs_0_.refs_4_, bf16[256,2048]{1,0:T(8,128)(2,1)} %get-tuple-element.52.refs_1_.refs_4_, bf16[2048,4096]{1,0:T(8,128)(2,1)} %refs_2_.3), custom_call_target="tpu_custom_call" | custom-call | flops 4294967296 | bytes 16777216 | tf_op jit(solution)/shard_map/second_part/pallas_call | solution.py:284
  186.5 20.8 %collective-permute-done.3.peer_ref = bf16[256,2048]{1,0:T(8,128)(2,1)S(1)} collective-permute-done((bf16[256,2048]{1,0:T(8,128)(2,1)}, bf16[256,2048]{1,0:T(8,128)(2,1)S(1)}, u32[]{:S(2)}, u32[]{:S(2)}) %collective-permute-start.3) | collective-permute-done | bytes 1048608 | tf_op jit(solution)/shard_map/ppermute | solution.py:920
  208.4 9.6 %middle_back.1 = (bf16[256,1024]{1,0:T(8,128)(2,1)}, f32[256,2048]{1,0:T(8,128)}, bf16[256,2048]{1,0:T(8,128)(2,1)}, f32[1,2048]{1,0:T(1,128)}, f32[1,2048]{1,0:T(1,128)}, /*index=5*/f32[1,2048]{1,0:T(1,128)}) custom-call(s32[3]{0:T(128)} %pad_add_fusion.pos, bf16[256,2048]{1,0:T(8,128)(2,1)} %second_part.1.own_ref, bf16[256,2048]{1,0:T(8,128)(2,1)} %copy-done.31, ...), custom_call_target="tpu_custom_call" | custom-call | flops 1073741824 | bytes 4194304 | tf_op jit(solution)/shard_map/middle_back/pallas_call | solution.py:284
  236.8 24.9 %spread3.1 = bf16[1,1024,256]{2,1,0:T(8,128)(2,1)} custom-call(bf16[1,256,1024]{2,1,0:T(8,128)(2,1)} %bitcast.64), custom_call_target="tpu_custom_call" | custom-call | tf_op jit(solution)/shard_map/spread3/pallas_call | solution.py:407
  270.7 46.0 %collect4.1.grads_ref = bf16[3,256,1024]{2,1,0:T(8,128)(2,1)} custom-call(bf16[3,1024,256]{2,1,0:T(8,128)(2,1)} %attend_back.1.src), custom_call_target="tpu_custom_call" | custom-call | tf_op jit(solution)/shard_map/collect4/pallas_call | solution.py:448
  320.5 12.7 %collective-permute-done.14.refs_5_ = bf16[256,1024]{1,0:T(8,128)(2,1)S(1)} collective-permute-done((bf16[256,1024]{1,0:T(8,128)(2,1)S(1)}, bf16[256,1024]{1,0:T(8,128)(2,1)S(1)}, u32[]{:S(2)}, u32[]{:S(2)}) %collective-permute-start.14) | collective-permute-done | bytes 524320 | tf_op jit(solution)/shard_map/ppermute | solution.py:920
  350.7 12.2 %collective-permute-done.11.refs_5_ = bf16[256,1024]{1,0:T(8,128)(2,1)S(1)} collective-permute-done((bf16[256,1024]{1,0:T(8,128)(2,1)S(1)}, bf16[256,1024]{1,0:T(8,128)(2,1)S(1)}, u32[]{:S(2)}, u32[]{:S(2)}) %collective-permute-start.11) | collective-permute-done | bytes 524320 | tf_op jit(solution)/shard_map/ppermute | solution.py:920
  371.6 12.2 %collective-permute-done.8.refs_5_ = bf16[256,1024]{1,0:T(8,128)(2,1)S(1)} collective-permute-done((bf16[256,1024]{1,0:T(8,128)(2,1)S(1)}, bf16[256,1024]{1,0:T(8,128)(2,1)S(1)}, u32[]{:S(2)}, u32[]{:S(2)}) %collective-permute-start.8) | collective-permute-done | bytes 524320 | tf_op jit(solution)/shard_map/ppermute | solution.py:920
  391.4 18.1 %collective-permute-done.38.refs_5_ = bf16[256,2048]{1,0:T(8,128)(2,1)} collective-permute-done((bf16[256,2048]{1,0:T(8,128)(2,1)S(1)}, bf16[256,2048]{1,0:T(8,128)(2,1)}, u32[]{:S(2)}, u32[]{:S(2)}) %collective-permute-start.38) | collective-permute-done | bytes 1048608 | tf_op jit(solution)/shard_map/ppermute | solution.py:920
  411.6 12.3 %collective-permute-done.32.refs_1_ = bf16[256,1024]{1,0:T(8,128)(2,1)S(1)} collective-permute-done((bf16[256,1024]{1,0:T(8,128)(2,1)S(1)}, bf16[256,1024]{1,0:T(8,128)(2,1)S(1)}, u32[]{:S(2)}, u32[]{:S(2)}) %collective-permute-start.32) | collective-permute-done | bytes 524320 | tf_op jit(solution)/shard_map/ppermute | solution.py:920
  436.5 23.5 %collective-permute-done.35.refs_5_ = bf16[256,2048]{1,0:T(8,128)(2,1)S(1)} collective-permute-done((bf16[256,2048]{1,0:T(8,128)(2,1)S(1)}, bf16[256,2048]{1,0:T(8,128)(2,1)S(1)}, u32[]{:S(2)}, u32[]{:S(2)}) %collective-permute-start.35) | collective-permute-done | bytes 1048608 | tf_op jit(solution)/shard_map/ppermute | solution.py:920
  472.6 23.5 %collective-permute-done.29.refs_5_ = bf16[256,2048]{1,0:T(8,128)(2,1)S(1)} collective-permute-done((bf16[256,2048]{1,0:T(8,128)(2,1)S(1)}, bf16[256,2048]{1,0:T(8,128)(2,1)S(1)}, u32[]{:S(2)}, u32[]{:S(2)}) %collective-permute-start.29) | collective-permute-done | bytes 1048608 | tf_op jit(solution)/shard_map/ppermute | solution.py:920
  498.2 12.3 %collective-permute-done.23.refs_1_ = bf16[256,1024]{1,0:T(8,128)(2,1)S(1)} collective-permute-done((bf16[256,1024]{1,0:T(8,128)(2,1)S(1)}, bf16[256,1024]{1,0:T(8,128)(2,1)S(1)}, u32[]{:S(2)}, u32[]{:S(2)}) %collective-permute-start.23) | collective-permute-done | bytes 524320 | tf_op jit(solution)/shard_map/ppermute | solution.py:920
  523.1 23.4 %collective-permute-done.26.refs_5_ = bf16[256,2048]{1,0:T(8,128)(2,1)S(1)} collective-permute-done((bf16[256,2048]{1,0:T(8,128)(2,1)S(1)}, bf16[256,2048]{1,0:T(8,128)(2,1)S(1)}, u32[]{:S(2)}, u32[]{:S(2)}) %collective-permute-start.26) | collective-permute-done | bytes 1048608 | tf_op jit(solution)/shard_map/ppermute | solution.py:920
  556.3 10.6 %reduced_part.1 = bf16[256,2048]{1,0:T(8,128)(2,1)} custom-call(s32[3]{0:T(128)} %pad_add_fusion.pos, bf16[256,2048]{1,0:T(8,128)(2,1)} %get-tuple-element.48.refs_0_.refs_4_, bf16[256,2048]{1,0:T(8,128)(2,1)} %get-tuple-element.49.refs_1_.refs_4_, bf16[4096,2048]{1,0:T(8,128)(2,1)} %refs_2_.2), custom_call_target="tpu_custom_call" | custom-call | flops 4294967296 | bytes 16777216 | tf_op jit(solution)/shard_map/reduced_part/pallas_call | solution.py:284
  578.9 14.4 %collective-permute-done.2 = bf16[256,2048]{1,0:T(8,128)(2,1)} collective-permute-done((bf16[256,2048]{1,0:T(8,128)(2,1)}, bf16[256,2048]{1,0:T(8,128)(2,1)}, u32[]{:S(2)}, u32[]{:S(2)}) %collective-permute-start.2) | collective-permute-done | bytes 1048608 | tf_op jit(solution)/shard_map/ppermute | solution.py:920
  596.0 19.0 %collective-permute-done.4.peer_ref = bf16[256,2048]{1,0:T(8,128)(2,1)} collective-permute-done((bf16[256,2048]{1,0:T(8,128)(2,1)}, bf16[256,2048]{1,0:T(8,128)(2,1)}, u32[]{:S(2)}, u32[]{:S(2)}) %collective-permute-start.4) | collective-permute-done | bytes 1048608 | tf_op jit(solution)/shard_map/ppermute | solution.py:920
  622.7 16.8 %totals.1 = f32[144,128]{1,0:T(8,128)} custom-call(f32[144,128]{1,0:T(8,128)} %copy-done.44), custom_call_target="tpu_custom_call" | custom-call | tf_op jit(solution)/shard_map/totals/pallas_call | solution.py:907
  (249 shorter events, 179.8 us)
Async XLA Ops:
  7.2 635.7 %reduce-scatter.15.cloned.1.call-start = ((), (), s32[]{:S(2)}) async-start(), calls=%async_computation.11 | async-start | bytes 1310720 | tf_op jit(solution)/shard_map/reduce_scatter | solution.py:1027
  9.0 48.7 %collective-permute-start = (bf16[512,2048]{1,0:T(8,128)(2,1)S(1)}, bf16[512,2048]{1,0:T(8,128)(2,1)S(1)}, u32[]{:S(2)}, u32[]{:S(2)}) collective-permute-start(bf16[512,2048]{1,0:T(8,128)(2,1)S(1)} %constant_dynamic-slice_fusion.12), channel_id=1, source_target_pairs={{0,16},{16,0},{1,17},{17,1},{2,18},{18,2},{3,19},{19,3},{4,20},{20... | collective-permute-start | bytes 6291464 | tf_op jit(solution)/shard_map/ppermute | solution.py:920
  57.6 85.0 %collective-permute-start.1 = (bf16[512,2048]{1,0:T(8,128)(2,1)S(1)}, bf16[512,2048]{1,0:T(8,128)(2,1)}, u32[]{:S(2)}, u32[]{:S(2)}) collective-permute-start(bf16[512,2048]{1,0:T(8,128)(2,1)S(1)} %collective-permute-done.near_ref), channel_id=1, source_target_pairs={{0,4},{4,0},{8,12},{12,8},{1,5},{5,1},{9,13},{13,9},{2,6},{6,2},{1... | collective-permute-start | bytes 6291464 | tf_op jit(solution)/shard_map/ppermute | solution.py:920
  184.6 22.8 %collective-permute-start.3 = (bf16[256,2048]{1,0:T(8,128)(2,1)}, bf16[256,2048]{1,0:T(8,128)(2,1)S(1)}, u32[]{:S(2)}, u32[]{:S(2)}) collective-permute-start(bf16[256,2048]{1,0:T(8,128)(2,1)} %second_part.1.own_ref), channel_id=1, source_target_pairs={{0,16},{16,0},{1,17},{17,1},{2,18},{18,2},{3,19},{19,3},{4,20},{20... | collective-permute-start | bytes 3145736 | tf_op jit(solution)/shard_map/ppermute | solution.py:920
  185.0 35.6 %collective-permute-start.20 = (bf16[256,1024]{1,0:T(8,128)(2,1)S(1)}, bf16[256,1024]{1,0:T(8,128)(2,1)S(1)}, u32[]{:S(2)}, u32[]{:S(2)}) collective-permute-start(bf16[256,1024]{1,0:T(8,128)(2,1)S(1)} %copy-done.32), channel_id=1, source_target_pairs={{0,8},{4,12},{8,0},{12,4},{1,9},{5,13},{9,1},{13,5},{2,10},{6,14},... | collective-permute-start | bytes 1572872 | tf_op jit(solution)/shard_map/ppermute | solution.py:920
  236.6 408.3 %reduce-scatter.13.cloned.1.call-start = ((), (), s32[]{:S(2)}) async-start(), calls=%async_computation.10 | async-start | bytes 1310720 | tf_op jit(solution)/shard_map/reduce_scatter | solution.py:1027
  320.2 21.5 %collective-permute-start.5 = (bf16[256,1024]{1,0:T(8,128)(2,1)S(1)}, bf16[256,1024]{1,0:T(8,128)(2,1)S(1)}, u32[]{:S(2)}, u32[]{:S(2)}) collective-permute-start(bf16[256,1024]{1,0:T(8,128)(2,1)S(1)} %constant_dynamic-slice_fusion.11), channel_id=1, source_target_pairs={{0,8},{4,12},{8,0},{12,4},{1,9},{5,13},{9,1},{13,5},{2,10},{6,14},... | collective-permute-start | bytes 1572872 | tf_op jit(solution)/shard_map/ppermute | solution.py:920
  320.5 22.8 %collective-permute-start.15 = (bf16[256,1024]{1,0:T(8,128)(2,1)S(1)}, bf16[256,1024]{1,0:T(8,128)(2,1)S(1)}, u32[]{:S(2)}, u32[]{:S(2)}) collective-permute-start(bf16[256,1024]{1,0:T(8,128)(2,1)S(1)} %get-tuple-element.85.refs_4_), channel_id=1, source_target_pairs={{0,4},{4,0},{8,12},{12,8},{1,5},{5,1},{9,13},{13,9},{2,6},{6,2},{1... | collective-permute-start | bytes 1572872 | tf_op jit(solution)/shard_map/ppermute | solution.py:920
  348.9 296.0 %reduce-scatter.11.cloned.1.call-start = ((), (), s32[]{:S(2)}) async-start(), calls=%async_computation.9 | async-start | bytes 1310720 | tf_op jit(solution)/shard_map/reduce_scatter | solution.py:1027
  369.7 275.1 %reduce-scatter.9.cloned.1.call-start = ((), (), s32[]{:S(2)}) async-start(), calls=%async_computation.8 | async-start | bytes 1310720 | tf_op jit(solution)/shard_map/reduce_scatter | solution.py:1027
  383.8 25.7 %collective-permute-start.38 = (bf16[256,2048]{1,0:T(8,128)(2,1)S(1)}, bf16[256,2048]{1,0:T(8,128)(2,1)}, u32[]{:S(2)}, u32[]{:S(2)}) collective-permute-start(bf16[256,2048]{1,0:T(8,128)(2,1)S(1)} %copy-done.6), channel_id=1, source_target_pairs={{0,8},{4,12},{8,0},{12,4},{1,9},{5,13},{9,1},{13,5},{2,10},{6,14},... | collective-permute-start | bytes 3145736 | tf_op jit(solution)/shard_map/ppermute | solution.py:920
  391.1 256.1 %reduce-scatter.23.cloned.1.call-start = ((), (), s32[]{:S(2)}) async-start(), calls=%async_computation.15 | async-start | bytes 2621440 | tf_op jit(solution)/shard_map/reduce_scatter | solution.py:1027
  391.2 34.4 %collective-permute-start.39 = (bf16[256,2048]{1,0:T(8,128)(2,1)S(1)}, bf16[256,2048]{1,0:T(8,128)(2,1)S(1)}, u32[]{:S(2)}, u32[]{:S(2)}) collective-permute-start(bf16[256,2048]{1,0:T(8,128)(2,1)S(1)} %copy-done.6), channel_id=1, source_target_pairs={{0,4},{4,0},{8,12},{12,8},{1,5},{5,1},{9,13},{13,9},{2,6},{6,2},{1... | collective-permute-start | bytes 3145736 | tf_op jit(solution)/shard_map/ppermute | solution.py:920
  433.5 213.7 %reduce-scatter.21.cloned.1.call-start = ((), (), s32[]{:S(2)}) async-start(), calls=%async_computation.14 | async-start | bytes 2621440 | tf_op jit(solution)/shard_map/reduce_scatter | solution.py:1027
  434.7 25.2 %collective-permute-start.35 = (bf16[256,2048]{1,0:T(8,128)(2,1)S(1)}, bf16[256,2048]{1,0:T(8,128)(2,1)S(1)}, u32[]{:S(2)}, u32[]{:S(2)}) collective-permute-start(bf16[256,2048]{1,0:T(8,128)(2,1)S(1)} %copy-done.5), channel_id=1, source_target_pairs={{0,8},{4,12},{8,0},{12,4},{1,9},{5,13},{9,1},{13,5},{2,10},{6,14},... | collective-permute-start | bytes 3145736 | tf_op jit(solution)/shard_map/ppermute | solution.py:920
  436.5 23.5 %collective-permute-start.36 = (bf16[256,2048]{1,0:T(8,128)(2,1)S(1)}, bf16[256,2048]{1,0:T(8,128)(2,1)S(1)}, u32[]{:S(2)}, u32[]{:S(2)}) collective-permute-start(bf16[256,2048]{1,0:T(8,128)(2,1)S(1)} %copy-done.5), channel_id=1, source_target_pairs={{0,4},{4,0},{8,12},{12,8},{1,5},{5,1},{9,13},{13,9},{2,6},{6,2},{1... | collective-permute-start | bytes 3145736 | tf_op jit(solution)/shard_map/ppermute | solution.py:920
  469.7 180.8 %reduce-scatter.19.cloned.1.call-start = ((), (), s32[]{:S(2)}) async-start(), calls=%async_computation.13 | async-start | bytes 2621440 | tf_op jit(solution)/shard_map/reduce_scatter | solution.py:1027
  470.9 25.2 %collective-permute-start.29 = (bf16[256,2048]{1,0:T(8,128)(2,1)S(1)}, bf16[256,2048]{1,0:T(8,128)(2,1)S(1)}, u32[]{:S(2)}, u32[]{:S(2)}) collective-permute-start(bf16[256,2048]{1,0:T(8,128)(2,1)S(1)} %copy-done.8), channel_id=1, source_target_pairs={{0,8},{4,12},{8,0},{12,4},{1,9},{5,13},{9,1},{13,5},{2,10},{6,14},... | collective-permute-start | bytes 3145736 | tf_op jit(solution)/shard_map/ppermute | solution.py:920
  472.6 39.5 %collective-permute-start.30 = (bf16[256,2048]{1,0:T(8,128)(2,1)S(1)}, bf16[256,2048]{1,0:T(8,128)(2,1)S(1)}, u32[]{:S(2)}, u32[]{:S(2)}) collective-permute-start(bf16[256,2048]{1,0:T(8,128)(2,1)S(1)} %copy-done.8), channel_id=1, source_target_pairs={{0,4},{4,0},{8,12},{12,8},{1,5},{5,1},{9,13},{13,9},{2,6},{6,2},{1... | collective-permute-start | bytes 3145736 | tf_op jit(solution)/shard_map/ppermute | solution.py:920
  520.2 130.2 %reduce-scatter.17.cloned.1.call-start = ((), (), s32[]{:S(2)}) async-start(), calls=%async_computation.12 | async-start | bytes 2621440 | tf_op jit(solution)/shard_map/reduce_scatter | solution.py:1027
  521.4 25.1 %collective-permute-start.26 = (bf16[256,2048]{1,0:T(8,128)(2,1)S(1)}, bf16[256,2048]{1,0:T(8,128)(2,1)S(1)}, u32[]{:S(2)}, u32[]{:S(2)}) collective-permute-start(bf16[256,2048]{1,0:T(8,128)(2,1)S(1)} %copy-done.7), channel_id=1, source_target_pairs={{0,8},{4,12},{8,0},{12,4},{1,9},{5,13},{9,1},{13,5},{2,10},{6,14},... | collective-permute-start | bytes 3145736 | tf_op jit(solution)/shard_map/ppermute | solution.py:920
  523.1 23.5 %collective-permute-start.27 = (bf16[256,2048]{1,0:T(8,128)(2,1)S(1)}, bf16[256,2048]{1,0:T(8,128)(2,1)S(1)}, u32[]{:S(2)}, u32[]{:S(2)}) collective-permute-start(bf16[256,2048]{1,0:T(8,128)(2,1)S(1)} %copy-done.7), channel_id=1, source_target_pairs={{0,4},{4,0},{8,12},{12,8},{1,5},{5,1},{9,13},{13,9},{2,6},{6,2},{1... | collective-permute-start | bytes 3145736 | tf_op jit(solution)/shard_map/ppermute | solution.py:920
  566.9 26.4 %collective-permute-start.2 = (bf16[256,2048]{1,0:T(8,128)(2,1)}, bf16[256,2048]{1,0:T(8,128)(2,1)}, u32[]{:S(2)}, u32[]{:S(2)}) collective-permute-start(bf16[256,2048]{1,0:T(8,128)(2,1)} %reduced_part.1), channel_id=1, source_target_pairs={{0,16},{16,0},{1,17},{17,1},{2,18},{18,2},{3,19},{19,3},{4,20},{20... | collective-permute-start | bytes 3145736 | tf_op jit(solution)/shard_map/ppermute | solution.py:920
  576.7 38.3 %collective-permute-start.4 = (bf16[256,2048]{1,0:T(8,128)(2,1)}, bf16[256,2048]{1,0:T(8,128)(2,1)}, u32[]{:S(2)}, u32[]{:S(2)}) collective-permute-start(bf16[256,2048]{1,0:T(8,128)(2,1)} %get-tuple-element.54.own_ref), channel_id=1, source_target_pairs={{0,16},{16,0},{1,17},{17,1},{2,18},{18,2},{3,19},{19,3},{4,20},{20... | collective-permute-start | bytes 3145736 | tf_op jit(solution)/shard_map/ppermute | solution.py:920
  (77 other events, 738.8 us)
Sparse Core Ops, SparseCore 0:
  236.7 36.9 reduce-scatter.14
  349.0 28.4 reduce-scatter.12
  379.8 25.7 reduce-scatter.10
  407.8 25.7 reduce-scatter.8
  435.7 42.7 reduce-scatter.22
  480.6 42.8 reduce-scatter.20
  525.8 42.8 reduce-scatter.18
  570.9 42.8 reduce-scatter.16
